TPU v7x, 32 devices: a whole 2x2x4 slice. The times are simulated.
32 devices in a mesh: row: 8 (over y, x, core), col: 4 (over z).
Axes of the slice: x: 2, y: 2, z: 4, core: 2. Of those that a mesh axis runs over, the one named last changes fastest.
Arguments:
- right_sides: float32 [8, 8192, 128], P(None, ('row', 'col')), may hold values from -6 to 6
- factor_head: bfloat16 [8, 8192, 4, 1024], P(None, 'row', None, 'col'), may hold values from -0.1875 to 0.1875
- class_head: int32 [8, 8, 4], P(None, 'row'), may hold values from 0 to 2
- scale_head: float32 [8, 8, 4], P(None, 'row'), may hold values from 0.25 to 2
- inverse_head: float32 [4, 1024, 1024], P(None, 'col'), as said below
- factor_tail: bfloat16 [4, 1024, 8, 8192], P(None, 'col', None, 'row'), may hold values from -0.1875 to 0.1875
- class_tail: int32 [4, 8, 8], P(None, None, 'row'), may hold values from 0 to 2
- scale_tail: float32 [4, 8, 8], P(None, None, 'row'), may hold values from 0.25 to 2
- inverse_tail: float32 [4, 1024, 1024], P(None, None, 'col'), as said below
Outputs:
- solved_head: float32 [4, 1024, 128], P(None, 'col')
- solved_tail: float32 [4, 1024, 128], P(None, 'col')
- remainder: float32 [8, 8192, 128], P(None, ('row', 'col'))
Inputs may be any that keep to these rules, and one draw needn't show every extreme that they name: `class_head`: 0, 1, 2 name the float32, bfloat16 and scaled bfloat16 classes. `class_tail`: 0, 1, 2 name the float32, bfloat16 and scaled bfloat16 classes. `inverse_head`: every tile is lower triangular with a diagonal of 1 to 2. `inverse_tail`: every tile is lower triangular with a diagonal of 1 to 2.
All inputs are finite; a program needn't handle non-finite values.
Results may differ from a plain program's by a relative error of at most 0.008.
Values sent between devices are 32-bit elements; how exact they have to be, the bound alone decides.
A program may use at most 128 MiB of HBM per device.

v0:
```python
import jax
import jax.numpy as jnp
from jax import lax
from jax.sharding import PartitionSpec as P


def from_root(block, axis, owner):
    block = jnp.where(lax.axis_index(axis) == owner, block, jnp.zeros_like(block))
    return lax.psum(block, axis)


def tile_terms(stored, classes, scales, solved, form):
    short_piece = solved.astype(jnp.bfloat16)
    exact_term = jnp.einsum(
        form, stored.astype(jnp.float32), solved, precision=lax.Precision.HIGHEST
    )
    short_term = jnp.einsum(form, stored, short_piece, preferred_element_type=jnp.float32)
    classes = classes[:, None, None]
    scales = scales[:, None, None]
    return jnp.where(
        classes == 0, exact_term, jnp.where(classes == 1, short_term, scales * short_term)
    )


def solve_tile(partial_value, right_share, owner_row, invert):
    share_rows = right_share.shape[0]
    placed = lax.dynamic_update_slice_in_dim(
        jnp.zeros(partial_value.shape, jnp.float32),
        right_share,
        lax.axis_index("col") * share_rows,
        0,
    )
    summed = lax.psum(partial_value - placed, "col")
    solved = invert(-summed)
    return from_root(solved, "row", owner_row)


def on_device(
    right_sides,
    factor_head,
    class_head,
    scale_head,
    inverse_head,
    factor_tail,
    class_tail,
    scale_tail,
    inverse_tail,
):
    n_row = lax.axis_size("row")
    slots = right_sides.shape[0]
    ntiles = slots * n_row
    window = inverse_head.shape[0]
    tile_rows = factor_head.shape[1]
    tile_ids = jnp.arange(slots, dtype=jnp.int32) * n_row + lax.axis_index("row")
    updates = jnp.zeros((slots, tile_rows, right_sides.shape[2]), jnp.float32)
    heads = []
    for step in range(window):
        slot_k, row_k = divmod(step, n_row)
        inverse_rows = inverse_head[step]

        def invert_head(value, inverse_rows=inverse_rows):
            return jnp.dot(
                inverse_rows,
                value,
                precision=lax.Precision.HIGHEST,
                preferred_element_type=jnp.float32,
            )

        solved = solve_tile(updates[slot_k], right_sides[slot_k], row_k, invert_head)
        heads.append(solved)
        terms = tile_terms(
            factor_head[:, :, step, :],
            class_head[:, 0, step],
            scale_head[:, 0, step],
            solved,
            "lab,bn->lan",
        )
        active = (tile_ids > step)[:, None, None]
        updates = updates + jnp.where(active, terms, jnp.float32(0.0))
    tails = [None] * window
    for step in range(window):
        target = ntiles - 1 - step
        position = window - 1 - step
        slot_j, row_j = divmod(target, n_row)
        inverse_cols = inverse_tail[position]

        def invert_tail(value, inverse_cols=inverse_cols):
            return jnp.dot(
                inverse_cols.T,
                value,
                precision=lax.Precision.HIGHEST,
                preferred_element_type=jnp.float32,
            )

        solved = solve_tile(updates[slot_j], right_sides[slot_j], row_j, invert_tail)
        tails[position] = solved
        terms = tile_terms(
            factor_tail[position],
            class_tail[position, :, 0],
            scale_tail[position, :, 0],
            solved,
            "alb,an->lbn",
        )
        active = (tile_ids < target)[:, None, None]
        updates = updates + jnp.where(active, terms, jnp.float32(0.0))
    summed = lax.psum_scatter(updates, "col", scatter_dimension=1, tiled=True)
    return (jnp.stack(heads), jnp.stack(tails), right_sides - summed)


def solution(mesh):
    return jax.shard_map(
        on_device,
        mesh=mesh,
        in_specs=(
            P(None, ("row", "col"), None),
            P(None, "row", None, "col"),
            P(None, "row", None),
            P(None, "row", None),
            P(None, "col", None),
            P(None, "col", None, "row"),
            P(None, None, "row"),
            P(None, None, "row"),
            P(None, None, "col"),
        ),
        out_specs=(P(None, "col", None), P(None, "col", None), P(None, ("row", "col"), None)),
        check_vma=False,
    )
```

profile of v0, /device:TPU:0, one launch (start us, length us, event | category | flops | bytes accessed | tf_op | source)
XLA Modules:
  0.0 989.1 jit_solution(2727695291262709679)
XLA Ops:
  9.8 41.2 %fusion.101 = (bf16[8,1024,1,256]{3,2,1,0:T(2,128)(2,1)}, bf16[8,1024,1,256]{3,2,1,0:T(2,128)(2,1)}, bf16[8,1024,1,256]{3,2,1,0:T(2,128)(2,1)}, bf16[8,1024,1,256]{3,2,1,0:T(2,128)(2,1)}) fusion(bf16[8,1024,4,256]{3,2,1,0:T(4,128)(2,1)} %param.10), kind=kLoop, calls=%fused_computation.170 | loop fusion | bytes 33554432 | tf_op jit(solution)/shard_map/slice | solution.py:72
  55.5 55.1 %all-reduce.19.cloned.1.call-done = f32[256,128]{0,1:T(8,128)} async-done(((f32[256,128]{0,1:T(8,128)}), f32[256,128]{0,1:T(8,128)}) %all-reduce.19.cloned.1.call-update) | async-done | bytes 131088 | tf_op jit(solution)/shard_map/psum | solution.py:9
  110.6 7.9 fusion.31
  123.0 38.1 %all-reduce.21.cloned.1.call-done = f32[1024,128]{0,1:T(8,128)} async-done(((f32[1024,128]{0,1:T(8,128)}), f32[1024,128]{0,1:T(8,128)}) %all-reduce.21.cloned.1.call-update) | async-done | bytes 524304 | tf_op jit(solution)/shard_map/psum | solution.py:33
  164.6 53.3 %all-reduce.23.cloned.1.call-done = f32[256,128]{0,1:T(8,128)} async-done(((f32[256,128]{0,1:T(8,128)}), f32[256,128]{0,1:T(8,128)}) %all-reduce.23.cloned.1.call-update) | async-done | bytes 131088 | tf_op jit(solution)/shard_map/psum | solution.py:9
  217.9 7.8 fusion.32
  225.7 5.0 fusion.4
  233.6 38.2 %all-reduce.25.cloned.1.call-done = f32[1024,128]{0,1:T(8,128)} async-done(((f32[1024,128]{0,1:T(8,128)}), f32[1024,128]{0,1:T(8,128)}) %all-reduce.25.cloned.1.call-update) | async-done | bytes 524304 | tf_op jit(solution)/shard_map/psum | solution.py:33
  275.1 53.5 %all-reduce.27.cloned.1.call-done = f32[256,128]{0,1:T(8,128)} async-done(((f32[256,128]{0,1:T(8,128)}), f32[256,128]{0,1:T(8,128)}) %all-reduce.27.cloned.1.call-update) | async-done | bytes 131088 | tf_op jit(solution)/shard_map/psum | solution.py:9
  328.6 7.8 fusion.33
  336.4 5.0 fusion.7
  344.5 38.0 %all-reduce.29.cloned.1.call-done = f32[1024,128]{0,1:T(8,128)} async-done(((f32[1024,128]{0,1:T(8,128)}), f32[1024,128]{0,1:T(8,128)}) %all-reduce.29.cloned.1.call-update) | async-done | bytes 524304 | tf_op jit(solution)/shard_map/psum | solution.py:33
  386.1 53.2 %all-reduce.31.cloned.1.call-done = f32[256,128]{0,1:T(8,128)} async-done(((f32[256,128]{0,1:T(8,128)}), f32[256,128]{0,1:T(8,128)}) %all-reduce.31.cloned.1.call-update) | async-done | bytes 131088 | tf_op jit(solution)/shard_map/psum | solution.py:9
  439.4 7.8 fusion.34
  455.0 12.3 %fusion.100 = (bf16[1,256,8,1024]{3,2,1,0:T(8,128)(2,1)}, bf16[1,256,8,1024]{3,2,1,0:T(8,128)(2,1)}, bf16[1,256,8,1024]{3,2,1,0:T(8,128)(2,1)}, bf16[1,256,8,1024]{3,2,1,0:T(8,128)(2,1)}) fusion(bf16[4,256,8,1024]{3,2,1,0:T(8,128)(2,1)} %param.14), kind=kLoop, calls=%fused_computation.169 | loop fusion | bytes 33554432 | tf_op jit(solution)/shard_map/slice | solution.py:98
  467.3 25.8 %all-reduce.33.cloned.1.call-done = f32[1024,128]{0,1:T(8,128)} async-done(((f32[1024,128]{0,1:T(8,128)}), f32[1024,128]{0,1:T(8,128)}) %all-reduce.33.cloned.1.call-update) | async-done | bytes 524304 | tf_op jit(solution)/shard_map/psum | solution.py:33
  495.9 54.0 %all-reduce.35.cloned.1.call-done = f32[256,128]{0,1:T(8,128)} async-done(((f32[256,128]{0,1:T(8,128)}), f32[256,128]{0,1:T(8,128)}) %all-reduce.35.cloned.1.call-update) | async-done | bytes 131088 | tf_op jit(solution)/shard_map/psum | solution.py:9
  549.9 7.3 fusion.23
  557.2 7.2 fusion.13
  567.4 38.0 %all-reduce.37.cloned.1.call-done = f32[1024,128]{0,1:T(8,128)} async-done(((f32[1024,128]{0,1:T(8,128)}), f32[1024,128]{0,1:T(8,128)}) %all-reduce.37.cloned.1.call-update) | async-done | bytes 524304 | tf_op jit(solution)/shard_map/psum | solution.py:33
  608.2 54.0 %all-reduce.39.cloned.1.call-done = f32[256,128]{0,1:T(8,128)} async-done(((f32[256,128]{0,1:T(8,128)}), f32[256,128]{0,1:T(8,128)}) %all-reduce.39.cloned.1.call-update) | async-done | bytes 131088 | tf_op jit(solution)/shard_map/psum | solution.py:9
  662.2 7.3 fusion.25
  669.6 7.2 fusion.16
  679.9 37.9 %all-reduce.41.cloned.1.call-done = f32[1024,128]{0,1:T(8,128)} async-done(((f32[1024,128]{0,1:T(8,128)}), f32[1024,128]{0,1:T(8,128)}) %all-reduce.41.cloned.1.call-update) | async-done | bytes 524304 | tf_op jit(solution)/shard_map/psum | solution.py:33
  720.5 54.0 %all-reduce.43.cloned.1.call-done = f32[256,128]{0,1:T(8,128)} async-done(((f32[256,128]{0,1:T(8,128)}), f32[256,128]{0,1:T(8,128)}) %all-reduce.43.cloned.1.call-update) | async-done | bytes 131088 | tf_op jit(solution)/shard_map/psum | solution.py:9
  774.5 7.3 fusion.27
  781.9 7.2 fusion.19
  792.3 37.9 %all-reduce.45.cloned.1.call-done = f32[1024,128]{0,1:T(8,128)} async-done(((f32[1024,128]{0,1:T(8,128)}), f32[1024,128]{0,1:T(8,128)}) %all-reduce.45.cloned.1.call-update) | async-done | bytes 524304 | tf_op jit(solution)/shard_map/psum | solution.py:33
  833.0 54.0 %all-reduce.47.cloned.1.call-done = f32[256,128]{0,1:T(8,128)} async-done(((f32[256,128]{0,1:T(8,128)}), f32[256,128]{0,1:T(8,128)}) %all-reduce.47.cloned.1.call-update) | async-done | bytes 131088 | tf_op jit(solution)/shard_map/psum | solution.py:9
  887.0 7.3 fusion.29
  894.3 8.8 fusion.22
  905.2 74.3 %reduce-scatter.2.cloned.1.call-done = f32[8,256,128]{1,2,0:T(8,128)} async-done(((f32[8,1024,128]{1,2,0:T(8,128)}), f32[8,256,128]{1,2,0:T(8,128)}) %reduce-scatter.2.cloned.1.call-update) | async-done | bytes 1048592 | tf_op jit(solution)/shard_map/reduce_scatter | solution.py:106
  (138 shorter events, 60.7 us)
Async XLA Ops:
  7.2 45.0 %all-reduce.17.cloned.1.call-start = ((), (), s32[]{:S(2)}) async-start(), calls=%async_computation.1 | async-start | bytes 1048576 | tf_op jit(solution)/shard_map/psum | solution.py:33
  9.7 41.3 %copy-start.29 = (f32[8,1,4]{0,2,1:T(4,128)S(1)}, f32[8,1,4]{0,2,1:T(4,128)}, u32[]{:S(2)}) copy-start(f32[8,1,4]{0,2,1:T(4,128)} %param.12) | copy-start | bytes 388
  9.7 41.3 %copy-start.27 = (s32[8,1,4]{0,2,1:T(4,128)S(1)}, s32[8,1,4]{0,2,1:T(4,128)}, u32[]{:S(2)}) copy-start(s32[8,1,4]{0,2,1:T(4,128)} %param.11) | copy-start | bytes 388
  9.7 100.9 %all-reduce.19.cloned.1.call-start = ((), (), s32[]{:S(2)}) async-start(), calls=%async_computation.2 | async-start | bytes 262144 | tf_op jit(solution)/shard_map/psum | solution.py:9
  55.4 105.7 %all-reduce.21.cloned.1.call-start = ((), (), s32[]{:S(2)}) async-start(), calls=%async_computation.3 | async-start | bytes 1048576 | tf_op jit(solution)/shard_map/psum | solution.py:33
  110.6 7.9 copy-start.4
  110.6 7.9 copy-start.19
  123.0 94.9 %all-reduce.23.cloned.1.call-start = ((), (), s32[]{:S(2)}) async-start(), calls=%async_computation.4 | async-start | bytes 262144 | tf_op jit(solution)/shard_map/psum | solution.py:9
  164.4 107.4 %all-reduce.25.cloned.1.call-start = ((), (), s32[]{:S(2)}) async-start(), calls=%async_computation.5 | async-start | bytes 1048576 | tf_op jit(solution)/shard_map/psum | solution.py:33
  217.9 7.8 copy-start.18
  217.9 7.8 copy-start.20
  233.6 95.0 %all-reduce.27.cloned.1.call-start = ((), (), s32[]{:S(2)}) async-start(), calls=%async_computation.6 | async-start | bytes 262144 | tf_op jit(solution)/shard_map/psum | solution.py:9
  275.0 107.4 %all-reduce.29.cloned.1.call-start = ((), (), s32[]{:S(2)}) async-start(), calls=%async_computation.7 | async-start | bytes 1048576 | tf_op jit(solution)/shard_map/psum | solution.py:33
  328.6 7.8 copy-start.12
  328.6 7.8 copy-start.21
  336.4 7.9 copy-start.30
  336.4 7.9 copy-start.28
  344.3 95.1 %all-reduce.31.cloned.1.call-start = ((), (), s32[]{:S(2)}) async-start(), calls=%async_computation.8 | async-start | bytes 262144 | tf_op jit(solution)/shard_map/psum | solution.py:9
  385.7 107.4 %all-reduce.33.cloned.1.call-start = ((), (), s32[]{:S(2)}) async-start(), calls=%async_computation.9 | async-start | bytes 1048576 | tf_op jit(solution)/shard_map/psum | solution.py:33
  439.4 7.8 copy-start.6
  439.4 7.8 copy-start.22
  455.0 94.9 %all-reduce.35.cloned.1.call-start = ((), (), s32[]{:S(2)}) async-start(), calls=%async_computation.10 | async-start | bytes 262144 | tf_op jit(solution)/shard_map/psum | solution.py:9
  495.8 109.6 %all-reduce.37.cloned.1.call-start = ((), (), s32[]{:S(2)}) async-start(), calls=%async_computation.11 | async-start | bytes 1048576 | tf_op jit(solution)/shard_map/psum | solution.py:33
  549.9 7.3 copy-start.23
  567.2 95.0 %all-reduce.39.cloned.1.call-start = ((), (), s32[]{:S(2)}) async-start(), calls=%async_computation.12 | async-start | bytes 262144 | tf_op jit(solution)/shard_map/psum | solution.py:9
  608.1 109.6 %all-reduce.41.cloned.1.call-start = ((), (), s32[]{:S(2)}) async-start(), calls=%async_computation.13 | async-start | bytes 1048576 | tf_op jit(solution)/shard_map/psum | solution.py:33
  662.2 7.3 copy-start.24
  679.6 94.9 %all-reduce.43.cloned.1.call-start = ((), (), s32[]{:S(2)}) async-start(), calls=%async_computation.14 | async-start | bytes 262144 | tf_op jit(solution)/shard_map/psum | solution.py:9
  720.5 109.7 %all-reduce.45.cloned.1.call-start = ((), (), s32[]{:S(2)}) async-start(), calls=%async_computation.15 | async-start | bytes 1048576 | tf_op jit(solution)/shard_map/psum | solution.py:33
  792.0 95.0 %all-reduce.47.cloned.1.call-start = ((), (), s32[]{:S(2)}) async-start(), calls=%async_computation.16 | async-start | bytes 262144 | tf_op jit(solution)/shard_map/psum | solution.py:9
  832.9 146.6 %reduce-scatter.2.cloned.1.call-start = ((), (), s32[]{:S(2)}) async-start(), calls=%async_computation.17 | async-start | bytes 5242880 | tf_op jit(solution)/shard_map/reduce_scatter | solution.py:106
  887.0 7.3 copy-start.26
  (16 other events, 79.9 us)
Sparse Core Ops, SparseCore 0:
  10.9 41.2 all-reduce.16
  55.8 54.7 all-reduce.18
  123.1 37.9 all-reduce.20
  164.6 53.2 all-reduce.22
  233.7 38.0 all-reduce.24
  275.3 53.2 all-reduce.26
  344.4 37.9 all-reduce.28
  386.0 53.2 all-reduce.30
  455.1 37.9 all-reduce.32
  496.6 53.2 all-reduce.34
  567.3 38.0 all-reduce.36
  608.9 53.2 all-reduce.38
  679.7 37.9 all-reduce.40
  721.2 53.2 all-reduce.42
  792.1 38.0 all-reduce.44
  833.6 53.2 all-reduce.46
  903.2 76.1 reduce-scatter.1
where the time goes:
time: 996 us; the launch traced here: 989 us
  waiting for transfers between devices  761 us (76%)
  matrix products  131 us (13%)
  local copies, waits for them, and re-layouts  72.4 us (7%)
  between operations  15 us (2%)
    psum x8, waiting for transfers between devices, from_root(): return lax.psum(block, axis)  431 us
    psum x8, waiting for transfers between devices, solve_tile(): summed = lax.psum(partial_value - placed, 'col')  255 us
    reduce_scatter x1, waiting for transfers between devices, on_device(): summed = lax.psum_scatter(updates, 'col', scatter_dimension=1, tiled=True)  74.3 us
    dot_general x8, matrix products, tile_terms(): jnp.einsum(form, stored.astype(jnp.float32), solved, precision=lax.Precis...  61.5 us
    dot_general x8, matrix products, tile_terms(): jnp.einsum(form, stored, short_piece, preferred_element_type=jnp.float32)  45.7 us
    slice x1, local copies, waits for them, and re-layouts, on_device(): factor_head[:, :, step, :]  41.2 us
  transfers between devices with their start and end apart: 17, of which 17 were waited for; matrix products, arithmetic and copies ran while one was open for 6% of the time, Pallas kernels for 0%

commit v1 on v0

v1 whole, which is shorter than its diff:
```python
import functools

import jax
import jax.numpy as jnp
from jax import lax
from jax.experimental import pallas as pl
from jax.experimental.pallas import tpu as pltpu
from jax.sharding import PartitionSpec as P

MESH = pl.DeviceIdType.MESH


def chain_kernel(
    n_row,
    n_col,
    coef_ref,
    right_ref,
    tiles_ref,
    inverse_head_ref,
    inverse_tail_ref,
    solved_out,
    solved,
    pair,
    part,
    sums,
    value,
    sum_send,
    sum_recv,
    value_send,
    value_recv,
    solved_send,
    solved_recv,
):
    window, share = inverse_head_ref.shape[0], inverse_head_ref.shape[1]
    columns = right_ref.shape[2]
    row, col = lax.axis_index("row"), lax.axis_index("col")

    def other_col(shift):
        return lax.rem(col + shift + n_col, n_col)

    def other_row(shift):
        return lax.rem(row + shift + n_row, n_row)

    barrier = pltpu.get_barrier_semaphore()
    for shift in range(1, n_col):
        pl.semaphore_signal(
            barrier, inc=1, device_id=(row, other_col(shift)), device_id_type=MESH
        )
    for shift in range(1, n_row):
        pl.semaphore_signal(
            barrier, inc=1, device_id=(other_row(shift), col), device_id_type=MESH
        )
    part[...] = jnp.zeros_like(part)
    pl.semaphore_wait(barrier, n_col + n_row - 2)

    def sum_copy(phase, shift):
        peer = other_col(shift)
        return pltpu.make_async_remote_copy(
            src_ref=part.at[phase, peer],
            dst_ref=sums.at[phase, shift - 1],
            send_sem=sum_send.at[phase, shift - 1],
            recv_sem=sum_recv.at[phase, shift - 1],
            device_id=(row, peer),
            device_id_type=MESH,
        )

    def value_copy(phase, shift):
        return pltpu.make_async_remote_copy(
            src_ref=value.at[phase, col],
            dst_ref=value.at[phase, col],
            send_sem=value_send.at[phase, shift - 1],
            recv_sem=value_recv.at[phase, shift - 1],
            device_id=(row, other_col(shift)),
            device_id_type=MESH,
        )

    def value_landed(phase, shift):
        source = other_col(-shift)
        return pltpu.make_async_remote_copy(
            src_ref=value.at[phase, source],
            dst_ref=value.at[phase, source],
            send_sem=value_send.at[phase, shift - 1],
            recv_sem=value_recv.at[phase, shift - 1],
            device_id=(row, source),
            device_id_type=MESH,
        )

    def solved_copy(index, shift):
        return pltpu.make_async_remote_copy(
            src_ref=solved.at[index],
            dst_ref=solved.at[index],
            send_sem=solved_send.at[index, shift - 1],
            recv_sem=solved_recv.at[index],
            device_id=(other_row(shift if index < window else -shift), col),
            device_id_type=MESH,
        )

    owners = [step for step in range(window)]
    owners += [n_row - 1 - step for step in range(window)]
    for index in range(2 * window):
        phase, step = divmod(index, window)
        position = step if phase == 0 else window - 1 - step
        inverse_ref = inverse_head_ref if phase == 0 else inverse_tail_ref

        @pl.when(row == owners[index])
        def _(index=index, phase=phase, position=position, inverse_ref=inverse_ref):
            total = right_ref[phase]
            if index > 0:
                for shift in range(1, n_col):
                    sum_copy(phase, shift).start()
                total = total - part[phase, col]
                for shift in range(1, n_col):
                    sum_copy(phase, shift).wait_recv()
                    total = total - sums[phase, shift - 1]
            value[phase, col] = total
            for shift in range(1, n_col):
                value_copy(phase, shift).start()

            def times(source):
                start = pl.multiple_of(source * share, share)
                return jnp.dot(
                    inverse_ref[position, :, pl.ds(start, share)],
                    value[phase, source],
                    precision=lax.Precision.HIGHEST,
                    preferred_element_type=jnp.float32,
                )

            result = times(col)
            for shift in range(1, n_col):
                value_landed(phase, shift).wait_recv()
                result = result + times(other_col(-shift))
            solved[index] = result
            for shift in range(1, n_row):
                solved_copy(index, shift).start()
            if index > 0:
                for shift in range(1, n_col):
                    sum_copy(phase, shift).wait_send()

        @pl.when(row != owners[index])
        def _(index=index):
            solved_copy(index, 1).wait_recv()

        if index == 2 * window - 1:
            break
        full = solved[index]
        high = full.astype(jnp.bfloat16)
        pair[:, :columns] = high
        pair[:, columns:] = (full - high.astype(jnp.float32)).astype(jnp.bfloat16)
        for kind in (0, 1) if phase == 0 else (2,):
            target = 0 if kind == 0 else 1
            high_coef = coef_ref[0, kind, position]
            low_coef = coef_ref[1, kind, position]

            def add_block(block, carry, kind=kind, target=target, high_coef=high_coef, low_coef=low_coef, position=position):
                product = jnp.dot(
                    tiles_ref[kind, position, block],
                    pair[...],
                    preferred_element_type=jnp.float32,
                )
                part[target, block] += (
                    high_coef * product[:, :columns] + low_coef * product[:, columns:]
                )
                return carry

            lax.fori_loop(0, n_col, add_block, 0)

    solved_out[...] = solved[...]
    for index in range(2 * window):

        @pl.when(row == owners[index])
        def _(index=index):
            for shift in range(1, n_col):
                value_copy(index // window, shift).wait_send()
            for shift in range(1, n_row):
                solved_copy(index, shift).wait_send()


def solve_chain(coefs, rights, tiles, inverse_head, inverse_tail, n_row, n_col):
    window, share = inverse_head.shape[:2]
    columns = rights.shape[2]
    piece = (share, columns)
    vmem = pl.BlockSpec(memory_space=pltpu.VMEM)
    dma = pltpu.SemaphoreType.DMA
    return pl.pallas_call(
        functools.partial(chain_kernel, n_row, n_col),
        out_shape=jax.ShapeDtypeStruct((2 * window,) + piece, jnp.float32),
        in_specs=[pl.BlockSpec(memory_space=pltpu.SMEM)] + [vmem] * 4,
        out_specs=vmem,
        scratch_shapes=[
            pltpu.VMEM((2 * window,) + piece, jnp.float32),
            pltpu.VMEM((share, 2 * columns), jnp.bfloat16),
            pltpu.VMEM((2, n_col) + piece, jnp.float32),
            pltpu.VMEM((2, n_col - 1) + piece, jnp.float32),
            pltpu.VMEM((2, n_col) + piece, jnp.float32),
            dma((2, n_col - 1)),
            dma((2, n_col - 1)),
            dma((2, n_col - 1)),
            dma((2, n_col - 1)),
            dma((2 * window, n_row - 1)),
            dma((2 * window,)),
        ],
        compiler_params=pltpu.CompilerParams(
            collective_id=0, has_side_effects=True, vmem_limit_bytes=40 * 2**20
        ),
    )(coefs, rights, tiles, inverse_head, inverse_tail)


def weighted_pairs(solved, classes, scales, active):
    classes, scales, active = (
        jnp.transpose(x)[:, :, None, None] for x in (classes, scales, active)
    )
    full = solved[None]
    short = lax.reduce_precision(full, 8, 7)
    piece = jnp.where(classes == 0, full, jnp.where(classes == 1, short, scales * short))
    piece = jnp.where(active, piece, jnp.float32(0.0))
    high = lax.reduce_precision(piece, 8, 7)
    return jnp.concatenate([high, piece - high], axis=3).astype(jnp.bfloat16)


def on_device(
    right_sides,
    factor_head,
    class_head,
    scale_head,
    inverse_head,
    factor_tail,
    class_tail,
    scale_tail,
    inverse_tail,
):
    n_row, n_col = lax.axis_size("row"), lax.axis_size("col")
    slots, share, columns = right_sides.shape
    ntiles = slots * n_row
    window = inverse_head.shape[0]
    tile_ids = jnp.arange(slots, dtype=jnp.int32) * n_row + lax.axis_index("row")
    steps = jnp.arange(window, dtype=jnp.int32)[:, None]
    head_class, head_scale = class_head[:, 0].T, scale_head[:, 0].T
    tail_class, tail_scale = class_tail[:, :, 0], scale_tail[:, :, 0]
    head_active = tile_ids[None, :] > steps
    tail_active = tile_ids[None, :] < ntiles - window + steps

    def coefs_of(classes, scales, active):
        high = jnp.where(active, jnp.where(classes == 2, scales, 1.0), 0.0)
        low = jnp.where(active, jnp.where(classes == 0, 1.0, 0.0), 0.0)
        return jnp.stack([high, low]).astype(jnp.float32)

    head_coefs = coefs_of(head_class, head_scale, head_active)
    tail_coefs = coefs_of(tail_class, tail_scale, tail_active)
    coefs = jnp.stack([head_coefs[:, :, 0], head_coefs[:, :, -1], tail_coefs[:, :, -1]], axis=1)
    tiles = jnp.stack(
        [
            jnp.transpose(factor_head[0], (1, 0, 2)),
            jnp.transpose(factor_head[-1], (1, 0, 2)),
            jnp.transpose(factor_tail[:, :, -1], (0, 2, 1)),
        ]
    ).reshape(3, window, n_col, share, share)
    rights = jnp.stack([right_sides[0], right_sides[-1]])
    solved = solve_chain(
        coefs,
        rights,
        tiles,
        inverse_head,
        jnp.transpose(inverse_tail, (0, 2, 1)),
        n_row,
        n_col,
    )
    heads, tails = solved[:window], solved[window:][::-1]
    head_pairs = weighted_pairs(heads, head_class, head_scale, head_active)
    tail_pairs = weighted_pairs(tails, tail_class, tail_scale, tail_active)
    updates = jnp.einsum(
        "lakb,lkbn->lan", factor_head, head_pairs, preferred_element_type=jnp.float32
    ) + jnp.einsum(
        "walb,lwan->lbn", factor_tail, tail_pairs, preferred_element_type=jnp.float32
    )
    updates = updates[:, :, :columns] + updates[:, :, columns:]
    summed = lax.psum_scatter(updates, "col", scatter_dimension=1, tiled=True)
    return heads, tails, right_sides - summed


def solution(mesh):
    return jax.shard_map(
        on_device,
        mesh=mesh,
        in_specs=(
            P(None, ("row", "col"), None),
            P(None, "row", None, "col"),
            P(None, "row", None),
            P(None, "row", None),
            P(None, "col", None),
            P(None, "col", None, "row"),
            P(None, None, "row"),
            P(None, None, "row"),
            P(None, None, "col"),
        ),
        out_specs=(P(None, "col", None), P(None, "col", None), P(None, ("row", "col"), None)),
        check_vma=False,
    )
```

time: 996 us -> 376 us (0.38)
  waiting for transfers between devices: 761 us -> 78.7 us
  Pallas kernels: 0 us -> 170 us
  matrix products: 131 us -> 44.8 us
  local copies, waits for them, and re-layouts: 72.4 us -> 35.6 us
  other arithmetic: 8.37 us -> 25.2 us
    psum x16 -> x0, waiting for transfers between devices: 686 us -> none  [the longest x8 431 us: from_root(): return lax.psum(block, axis)]
    pallas_call x0 -> x1, Pallas kernels: none -> 170 us  [solve_chain(): pl.pallas_call(functools.partial(chain_kernel, n_row, n_col), out_shape=j...]
    dot_general x24 -> x2, matrix products: 131 us -> 44.8 us  [the longest x1 29.6 us: on_device(): jnp.einsum('walb,lwan->lbn', factor_tail, tail_pairs, preferred_element_t...]
    slice x2, local copies, waits for them, and re-layouts: 53.5 us -> 1.18 us  [the longest x1 0.99 us: on_device(): rights = jnp.stack([right_sides[0], right_sides[-1]])]
    another operation x2 -> x6, other arithmetic: 0.07 us -> 14.9 us  [on_device(): return (jnp.stack(heads), jnp.stack(tails), right_sides - summed)]
    unnamed x66 -> x22, local copies, waits for them, and re-layouts: 18.7 us -> 24.3 us
  transfers between devices with their start and end apart: 17 -> 1, of which waited for: 17 -> 1; matrix products, arithmetic and copies ran while one was open for 6% -> 0% of each run, Pallas kernels for 0% -> 0%
where the time goes in v1:
time: 376 us; the launch traced here: 369 us
  Pallas kernels  170 us (45%)
  waiting for transfers between devices  78.7 us (21%)
  matrix products  44.8 us (12%)
  local copies, waits for them, and re-layouts  35.6 us (9%)
  other arithmetic  25.2 us (7%)
  between operations  14.7 us (4%)
    pallas_call x1, Pallas kernels, solve_chain(): pl.pallas_call(functools.partial(chain_kernel, n_row, n_col), out_shape=j...  170 us
    reduce_scatter x1, waiting for transfers between devices, on_device(): summed = lax.psum_scatter(updates, 'col', scatter_dimension=1, tiled=True)  78.7 us
    dot_general x1, matrix products, on_device(): jnp.einsum('walb,lwan->lbn', factor_tail, tail_pairs, preferred_element_t...  29.6 us
    unnamed x22, local copies, waits for them, and re-layouts  24.3 us
    dot_general x1, matrix products, on_device(): jnp.einsum('lakb,lkbn->lan', factor_head, head_pairs, preferred_element_t...  15.2 us
    another operation x2, other arithmetic  7.91 us
  transfers between devices with their start and end apart: 1, of which 1 were waited for; matrix products, arithmetic and copies ran while one was open for 0% of the time, Pallas kernels for 0%

profile of v1, /device:TPU:0, one launch (start us, length us, event | category | flops | bytes accessed | tf_op | source)
XLA Modules:
  0.0 368.9 jit_solution(1125377680795580865)
XLA Ops:
  7.2 0.7 broadcast_compare_fusion.2
  7.9 0.7 compare_select_fusion
  8.6 1.0 fusion.25
  9.6 15.4 %copy.38 = bf16[4,256,8,1024]{3,1,0,2:T(8,128)(2,1)S(1)} copy(bf16[4,256,8,1024]{3,2,1,0:T(8,128)(2,1)} %param.14) | data formatting | bytes 33554432 | tf_op args[5]
  25.0 0.2 slice_bitcast_fusion
  25.2 2.6 copy.39
  27.8 3.0 slice_bitcast_fusion.2
  30.8 1.6 copy.37
  32.4 1.6 copy.36
  34.0 5.6 %copy.40 = f32[4,1024,256]{1,2,0:T(8,128)} copy(f32[4,1024,256]{2,1,0:T(8,128)} %param.17) | data formatting | bytes 8388608 | tf_op args[8]
  39.8 0.2 fusion.16
  39.9 0.2 maximum_reduce_fusion
  40.2 7.0 %pad_maximum_fusion.tiles_ref = bf16[3,4,4,256,256]{4,3,2,1,0:T(8,128)(2,1)} fusion(bf16[1,4,4,256,256]{4,3,2,1,0:T(8,128)(2,1)S(1)} %bitcast.70, bf16[1,4,4,256,256]{4,3,2,1,0:T(8,128)(2,1)} %bitcast.71, bf16[1,4,4,256,256]{4,3,2,1,0:T(8,128)(2,1)} %bitcast.72), kind=kLoop, calls=%fused_computation.4 | loop fusion | flops 6291456 | bytes 12582912 | tf_op jit(solution)/shard_map/stack | solution.py:250
  47.2 170.0 %shard_map.112 = f32[8,256,128]{2,1,0:T(8,128)S(1)} custom-call(f32[2,3,4]{2,1,0:T(4,128)S(1)} %pad_maximum_fusion.4.coef_ref, f32[2,256,128]{2,1,0:T(8,128)S(1)} %pad_maximum_fusion.1.right_ref, bf16[3,4,4,256,256]{4,3,2,1,0:T(8,128)(2,1)} %pad_maximum_fusion.tiles_ref, f32[4,256,1024]{2,1,0:T(8,128)S(1)} %copy-done.1, f32[4,256,1024]{2,1,0:T(8,128)S(1)} %bitcast.69), custom_call_target="tpu_custom_call" | custom-call | tf_op jit(solution)/shard_map/pallas_call | solution.py:184
  217.2 0.1 fusion.23
  217.4 0.4 copy-done.7
  217.9 0.2 copy.50
  218.1 0.2 copy.48
  218.3 0.1 copy.49
  218.6 0.2 copy.44
  218.8 0.2 copy.42
  219.0 0.1 copy.43
  219.2 3.8 %reduce-precision_convert_fusion = (bf16[8,4,256,128]{2,3,1,0:T(8,128)(2,1)}, bf16[8,4,256,128]{2,3,1,0:T(8,128)(2,1)}) fusion(f32[8,4]{1,0:T(8,128)S(1)} %copy.51, f32[4,256,128]{1,2,0:T(8,128)S(1)} %copy.50, f32[4,256,128]{1,2,0:T(8,128)S(1)} %copy.48, pred[8,4]{1,0:T(8,128)(4,1)S(1)} %copy.49, pred[8,4]{1,0:T(8,128)(4,1)S(1)} %copy.47, ...), kind=kLoop, calls=%fused_computation.6 | loop fusion | flops 8388608 | bytes 5243104 | tf_op jit(solution)/shard_map/convert
  223.1 29.6 %fusion.8 = f32[8,256,1024,1]{2,1,3,0:T(8,128)} fusion(bf16[8,4,256,128]{2,3,1,0:T(8,128)(2,1)} %get-tuple-element.22, bf16[8,4,256,128]{2,3,1,0:T(8,128)(2,1)} %get-tuple-element.21, bf16[4,256,8,1024]{3,2,1,0:T(8,128)(2,1)} %param.14), kind=kOutput, calls=%fused_computation.15 | convolution fusion | flops 4303355904 | bytes 29360128 | tf_op jit(solution)/shard_map/walb,lwan->lbn/dot_general | solution.py:272
  252.7 4.1 %reduce-precision_convert_fusion.1 = (bf16[8,4,256,128]{2,3,1,0:T(8,128)(2,1)}, bf16[8,4,256,128]{2,3,1,0:T(8,128)(2,1)}) fusion(f32[8,4]{1,0:T(8,128)S(1)} %copy.45, f32[4,256,128]{1,2,0:T(8,128)S(1)} %copy.44, f32[4,256,128]{1,2,0:T(8,128)S(1)} %copy.42, pred[8,4]{1,0:T(8,128)(4,1)S(1)} %copy.43, pred[8,4]{1,0:T(8,128)(4,1)S(1)} %copy.41, ...), kind=kLoop, calls=%fused_computation.8 | loop fusion | flops 8388608 | bytes 5243104 | tf_op jit(solution)/shard_map/convert.2
  256.8 15.2 %fusion.2 = f32[8,1024,256]{1,2,0:T(8,128)} fusion(f32[8,256,1024,1]{2,1,3,0:T(8,128)} %fusion.8, bf16[8,1024,4,256]{3,2,1,0:T(4,128)(2,1)} %param.10, bf16[8,4,256,128]{2,3,1,0:T(8,128)(2,1)} %get-tuple-element.20, bf16[8,4,256,128]{2,3,1,0:T(8,128)(2,1)} %get-tuple-element.19), kind=kOutput, calls=%fused_computation.3 | convolution fusion | flops 4305453056 | bytes 37748736 | tf_op jit(solution)/shard_map/lakb,lkbn->lan/dot_general | solution.py:270
  271.9 6.8 %slice_add_fusion = f32[8,1024,128]{1,2,0:T(8,128)} fusion(f32[8,1024,256]{1,2,0:T(8,128)} %fusion.2), kind=kLoop, calls=%fused_computation.11 | loop fusion | flops 1048576 | bytes 12582912 | tf_op jit(solution)/shard_map/add | solution.py:275
  278.8 1.2 copy-done.5
  280.0 0.3 copy.53
  280.3 78.7 %reduce-scatter.2.cloned.1.call-done = f32[8,256,128]{1,2,0:T(8,128)} async-done(((f32[8,1024,128]{1,2,0:T(8,128)}), f32[8,256,128]{1,2,0:T(8,128)}) %reduce-scatter.2.cloned.1.call-update) | async-done | bytes 1048592 | tf_op jit(solution)/shard_map/reduce_scatter | solution.py:276
  359.0 1.4 sub.11
  360.3 1.3 copy.54
  (32 shorter events, 0.7 us)
Async XLA Ops:
  7.2 351.8 %reduce-scatter.2.cloned.1.call-start = ((), (), s32[]{:S(2)}) async-start(), calls=%async_computation.1 | async-start | bytes 5242880 | tf_op jit(solution)/shard_map/reduce_scatter | solution.py:276
  34.0 5.6 %copy-start.6 = (s32[8,1,4]{0,2,1:T(4,128)S(1)}, s32[8,1,4]{0,2,1:T(4,128)}, u32[]{:S(2)}) copy-start(s32[8,1,4]{0,2,1:T(4,128)} %param.11) | copy-start | bytes 388
  34.0 5.6 %copy-start.8 = (f32[8,1,4]{0,2,1:T(4,128)S(1)}, f32[8,1,4]{0,2,1:T(4,128)}, u32[]{:S(2)}) copy-start(f32[8,1,4]{0,2,1:T(4,128)} %param.12) | copy-start | bytes 388
  34.0 6.1 %copy-start.2 = (bf16[4,1024,256]{2,1,0:T(8,128)(2,1)S(1)}, bf16[4,1024,256]{2,1,0:T(8,128)(2,1)}, u32[]{:S(2)}) copy-start(bf16[4,1024,256]{2,1,0:T(8,128)(2,1)} %copy.39) | copy-start | bytes 6291460
  40.1 7.0 %copy-start = (f32[4,1024,256]{1,2,0:T(8,128)S(1)}, f32[4,1024,256]{1,2,0:T(8,128)}, u32[]{:S(2)}) copy-start(f32[4,1024,256]{1,2,0:T(8,128)} %copy.40) | copy-start | bytes 12582916
  40.1 7.0 %copy-start.1 = (f32[4,256,1024]{2,1,0:T(8,128)S(1)}, f32[4,256,1024]{2,1,0:T(8,128)}, u32[]{:S(2)}) copy-start(f32[4,256,1024]{2,1,0:T(8,128)} %inverse_head_ref.1) | copy-start | bytes 12582916
  217.2 0.7 copy-start.7
  217.3 5.7 %copy-start.3 = (f32[4,256,128]{2,1,0:T(8,128)}, f32[4,256,128]{2,1,0:T(8,128)S(1)}, u32[]{:S(2)}) copy-start(f32[4,256,128]{2,1,0:T(8,128)S(1)} %get-tuple-element.12) | copy-start | bytes 1572868
  217.4 5.7 %copy-start.4 = (f32[4,256,128]{2,1,0:T(8,128)}, f32[4,256,128]{2,1,0:T(8,128)S(1)}, u32[]{:S(2)}) copy-start(f32[4,256,128]{2,1,0:T(8,128)S(1)} %get-tuple-element.14) | copy-start | bytes 1572868
  278.7 1.2 copy-start.5
Sparse Core Ops, SparseCore 0:
  278.9 80.0 reduce-scatter.1
